TPU v7x, 32 devices: a whole 2x2x4 slice. The times are simulated.
32 devices in a mesh: row: 8 (over z, x), col: 4 (over y, core).
Axes of the slice: x: 2, y: 2, z: 4, core: 2. Of those that a mesh axis runs over, the one named last changes fastest.
Arguments:
- curvature: float32 [32, 1024, 4096], P(None, 'row', 'col'), may hold values from -4 to 7, as said below
Outputs:
- factored: float32 [32, 1024, 4096], P(None, 'row', 'col')
Inputs may be any that keep to these rules, and one draw needn't show every extreme that they name: `curvature`: rows 0 to 4095, read as a square matrix, are symmetric positive definite with smallest eigenvalue at least 0.5.
All inputs are finite; a program needn't handle non-finite values.
Results may differ from a plain program's by a relative error of at most 0.0014.
Values may be sent and summed in bfloat16 or wider, within the bound.
A program may use at most 192 MiB of HBM per device.

v0:
```python
import jax
import jax.numpy as jnp
from jax import lax
from jax.sharding import PartitionSpec as P

BLOCK = 128
HIGH = lax.Precision.HIGH
HIGHEST = lax.Precision.HIGHEST


def from_root(x, axis, root):
    mine = lax.axis_index(axis) == root
    return lax.psum(jnp.where(mine, x, jnp.zeros_like(x)), axis)


def nt(left, right, precision=None):
    return lax.dot_general(
        left,
        right,
        (((1,), (1,)), ((), ())),
        precision=precision,
        preferred_element_type=jnp.float32,
    )


def nn(left, right):
    return lax.dot_general(
        left, right, (((1,), (0,)), ((), ())), precision=HIGHEST, preferred_element_type=jnp.float32
    )


def factor_and_inverse(block):
    n = block.shape[0]
    width = min(BLOCK, n)
    rest = 0.5 * (block + block.T)
    identity = jnp.eye(width, dtype=jnp.float32)
    columns, inverses = ([], [])
    for start in range(0, n, width):
        small = lax.linalg.cholesky(rest[:width, :width], symmetrize_input=False)
        inverse = jax.scipy.linalg.solve_triangular(small, identity, lower=True)
        inverses.append(inverse)
        pieces = [jnp.zeros((start, width), jnp.float32)] if start else []
        pieces.append(small)
        if start + width < n:
            below = nt(rest[width:, :width], inverse, HIGHEST)
            rest = rest[width:, width:] - nt(below, below, HIGHEST)
            pieces.append(below)
        columns.append(jnp.concatenate(pieces, 0))
    factor = jnp.concatenate(columns, 1)
    size = width
    while len(inverses) > 1:
        merged = []
        for i in range(0, len(inverses), 2):
            top, bottom = (inverses[i], inverses[i + 1])
            at = i * size
            corner = factor[at + size : at + 2 * size, at : at + size]
            left = -nn(bottom, nn(corner, top))
            merged.append(
                jnp.concatenate(
                    [
                        jnp.concatenate([top, jnp.zeros_like(top)], 1),
                        jnp.concatenate([left, bottom], 1),
                    ],
                    0,
                )
            )
        inverses = merged
        size *= 2
    return (factor, inverses[0])


def on_device(curvature):
    cycles, tile, width = curvature.shape
    row = lax.axis_index("row")
    col = lax.axis_index("col")

    def gather_rows(piece):
        return lax.all_gather(piece, "row", axis=0, tiled=True)

    def own_rows(matrix):
        return lax.dynamic_slice_in_dim(matrix, row * tile, tile, 0)

    block00 = gather_rows(from_root(curvature[0], "col", 0))
    head = from_root(jnp.stack([curvature[0], curvature[1]], 0), "col", 1)
    block01 = gather_rows(head[0])
    block11 = gather_rows(head[1])
    mine0 = gather_rows(curvature[0])
    mine1 = gather_rows(curvature[1])
    factor0, inverse0 = factor_and_inverse(block00)
    below = curvature[1:].reshape((cycles - 1) * tile, width)
    solved0 = nt(below, inverse0, HIGH)
    sent0 = solved0.astype(jnp.bfloat16)
    sent0, block11, block01 = lax.optimization_barrier((sent0, block11, block01))
    panel0 = from_root(sent0, "col", 0)
    next0 = nn(inverse0, block01).astype(jnp.bfloat16)
    facing0 = nn(inverse0, mine0).astype(jnp.bfloat16)

    def tn(left, right):
        return lax.dot_general(
            left, right, (((0,), (0,)), ((), ())), preferred_element_type=jnp.float32
        )

    factor1, inverse1 = factor_and_inverse(block11 - tn(next0, next0))
    facing1 = nn(inverse1, mine1 - tn(next0, facing0)).astype(jnp.bfloat16)

    def plain(left, right):
        return lax.dot_general(
            left, right, (((1,), (0,)), ((), ())), preferred_element_type=jnp.float32
        )

    state = jnp.where(col == 0, solved0, below - plain(panel0, facing0))
    low = state[tile:]
    solved1 = nt(low, inverse1, HIGH)
    panel1 = from_root(solved1.astype(jnp.bfloat16), "col", 1)
    low = jnp.where(col == 1, solved1, jnp.where(col > 1, low - plain(panel1, facing1), low))
    zeros = jnp.zeros((tile, width), jnp.float32)
    first = jnp.where(col == 0, own_rows(factor0), zeros)
    second = jnp.where(col == 0, state[:tile], jnp.where(col == 1, own_rows(factor1), zeros))
    return jnp.concatenate([first, second, low], 0).reshape(cycles, tile, width)


def solution(mesh):
    in_specs = (P(None, "row", "col"),)
    out_specs = P(None, "row", "col")
    return jax.shard_map(
        on_device, mesh=mesh, in_specs=in_specs, out_specs=out_specs, check_vma=False
    )
```

profile of v0, /device:TPU:1, one launch (start us, length us, event | category | flops | bytes accessed | tf_op | source)
XLA Modules:
  0.0 980.9 jit_solution(16894256061563243643)
XLA Ops:
  6.5 2.2 fusion.245
  11.2 45.0 %all-reduce.25.cloned.1.call-done = (f32[128,1024]{0,1:T(8,128)}, f32[2,128,1024]{1,2,0:T(8,128)}) async-done(((f32[128,1024]{0,1:T(8,128)}, f32[2,128,1024]{1,2,0:T(8,128)}), (f32[128,1024]{0,1:T(8,128)}, f32[2,128,1024]{1,2,0:T(8,128)})) %all-reduce.25.cloned.1.call-update) | async-done | bytes 1572880 | tf_op jit(solution)/shard_map/psum | solution.py:13
  56.3 2.2 fusion.246
  59.8 11.9 %slice.227 = f32[31,128,1024]{2,1,0:T(8,128)} slice(f32[32,128,1024]{2,1,0:T(8,128)} %param.4), slice={[1:32], [0:128], [0:1024]} | slice | bytes 32505856 | tf_op jit(solution)/shard_map/slice | solution.py:90
  71.7 60.6 %all-gather.10.cloned.1.call-done = f32[1024,1024]{0,1:T(8,128)} async-done(((f32[128,1024]{0,1:T(8,128)}), f32[1024,1024]{0,1:T(8,128)}) %all-gather.10.cloned.1.call-update) | async-done | bytes 4194320 | tf_op jit(solution)/shard_map/all_gather | solution.py:78
  132.3 5.3 copy.3
  137.6 4.5 fusion.7
  144.2 11.7 %custom-call.36 = f32[128,128]{1,0:T(8,128)S(1)} custom-call(f32[128,128]{1,0:T(8,128)S(1)} %slice.260), custom_call_target="Cholesky" | custom-call | tf_op jit(solution)/shard_map/cholesky/custom-call.1 | solution.py:39
  157.2 9.8 custom-call.37
  168.8 4.9 slice_subtract_fusion.1
  175.5 12.0 %custom-call.38 = f32[128,128]{1,0:T(8,128)S(1)} custom-call(f32[128,128]{1,0:T(8,128)S(1)} %slice.263), custom_call_target="Cholesky" | custom-call | tf_op jit(solution)/shard_map/cholesky/custom-call.1 | solution.py:39
  189.0 9.8 custom-call.39
  200.6 3.7 slice_subtract_fusion.3
  205.7 11.7 %custom-call.40 = f32[128,128]{1,0:T(8,128)S(1)} custom-call(f32[128,128]{1,0:T(8,128)S(1)} %slice.266), custom_call_target="Cholesky" | custom-call | tf_op jit(solution)/shard_map/cholesky/custom-call.1 | solution.py:39
  219.4 10.0 %custom-call.41 = f32[1,128,128]{1,2,0:T(8,128)S(1)} custom-call(f32[1,128,128]{2,1,0:T(8,128)S(1)} %get-tuple-element.41), custom_call_target="InvertDiagBlocksLowerTriangular" | custom-call | tf_op jit(solution)/shard_map/jit(_solve_triangular)/triangular_solve | solution.py:40
  231.1 2.9 slice_subtract_fusion.5
  235.1 11.7 %custom-call.42 = f32[128,128]{1,0:T(8,128)S(1)} custom-call(f32[128,128]{1,0:T(8,128)S(1)} %slice.269), custom_call_target="Cholesky" | custom-call | tf_op jit(solution)/shard_map/cholesky/custom-call.1 | solution.py:39
  248.9 9.8 custom-call.43
  260.3 2.2 convolution_subtract_fusion.2
  262.6 11.9 %custom-call.44 = f32[128,128]{1,0:T(8,128)S(1)} custom-call(f32[128,128]{1,0:T(8,128)S(1)} %slice.272), custom_call_target="Cholesky" | custom-call | tf_op jit(solution)/shard_map/cholesky/custom-call.1 | solution.py:39
  275.8 9.8 custom-call.45
  289.7 11.7 %custom-call.46 = f32[128,128]{1,0:T(8,128)S(1)} custom-call(f32[128,128]{1,0:T(8,128)S(1)} %slice.275), custom_call_target="Cholesky" | custom-call | tf_op jit(solution)/shard_map/cholesky/custom-call.1 | solution.py:39
  302.7 9.8 custom-call.47
  315.7 11.7 %custom-call.48 = f32[128,128]{1,0:T(8,128)S(1)} custom-call(f32[128,128]{1,0:T(8,128)S(1)} %slice.278), custom_call_target="Cholesky" | custom-call | tf_op jit(solution)/shard_map/cholesky/custom-call.1 | solution.py:39
  329.4 9.8 custom-call.49
  340.1 11.7 %custom-call.50 = f32[128,128]{1,0:T(8,128)S(1)} custom-call(f32[128,128]{1,0:T(8,128)S(1)} %convolution_subtract_fusion.8), custom_call_target="Cholesky" | custom-call | tf_op jit(solution)/shard_map/cholesky/custom-call.1 | solution.py:39
  355.2 9.9 %custom-call.51 = f32[1,128,128]{1,2,0:T(8,128)S(1)} custom-call(f32[1,128,128]{2,1,0:T(8,128)S(1)} %get-tuple-element.31), custom_call_target="InvertDiagBlocksLowerTriangular" | custom-call | tf_op jit(solution)/shard_map/jit(_solve_triangular)/triangular_solve | solution.py:40
  376.0 31.0 %bitcast_convert_fusion = (bf16[3968,1024]{1,0:T(8,128)(2,1)}, f32[1024,3968]{0,1:T(8,128)}) fusion(f32[3968,1024]{1,0:T(8,128)} %bitcast.189, f32[512,512]{1,0:T(8,128)S(1)} %select_maximum_fusion.3, f32[128,128]{1,0:T(8,128)S(1)} %copy-done.83, f32[128,128]{1,0:T(8,128)S(1)} %convolution_negate_fusion.10, f32[128,256]{1,0:T(8,128)S(1)} %copy-done.64, ...), kind=kOutput, calls=%fused_computation.3 | convolution fusion | flops 24976949248 | bytes 43778048 | tf_op jit(solution)/shard_map/dot_general | solution.py:17
  407.0 3.8 broadcast_select_fusion
  411.7 19.4 %convolution_convert_fusion = bf16[1024,1024]{1,0:T(8,128)(2,1)S(1)} fusion(f32[1024,1024]{0,1:T(8,128)} %bitcast.192, f32[512,512]{1,0:T(8,128)} %copy-done.31, f32[128,128]{1,0:T(8,128)S(1)} %copy-done.84, f32[128,128]{1,0:T(8,128)S(1)} %convolution_negate_fusion.10, f32[128,256]{1,0:T(8,128)S(1)} %copy-done.65, ...), kind=kOutput, calls=%fused_computation.27 | convolution fusion | flops 12894339072 | bytes 9437184 | tf_op jit(solution)/shard_map/dot_general | solution.py:27
  432.5 4.5 convolution_subtract_fusion
  437.1 5.6 copy.18
  442.7 4.6 fusion.4
  449.4 11.7 %custom-call.52 = f32[128,128]{1,0:T(8,128)S(1)} custom-call(f32[128,128]{1,0:T(8,128)S(1)} %slice.287), custom_call_target="Cholesky" | custom-call | tf_op jit(solution)/shard_map/cholesky/custom-call.1 | solution.py:39
  462.9 9.8 custom-call.53
  474.6 4.8 slice_subtract_fusion
  481.1 11.9 %custom-call.54 = f32[128,128]{1,0:T(8,128)S(1)} custom-call(f32[128,128]{1,0:T(8,128)S(1)} %slice.290), custom_call_target="Cholesky" | custom-call | tf_op jit(solution)/shard_map/cholesky/custom-call.1 | solution.py:39
  495.1 9.8 custom-call.55
  507.4 3.7 slice_subtract_fusion.2
  512.5 11.7 %custom-call.56 = f32[128,128]{1,0:T(8,128)S(1)} custom-call(f32[128,128]{1,0:T(8,128)S(1)} %slice.293), custom_call_target="Cholesky" | custom-call | tf_op jit(solution)/shard_map/cholesky/custom-call.1 | solution.py:39
  526.2 10.2 %custom-call.57 = f32[1,128,128]{1,2,0:T(8,128)S(1)} custom-call(f32[1,128,128]{2,1,0:T(8,128)S(1)} %get-tuple-element.25), custom_call_target="InvertDiagBlocksLowerTriangular" | custom-call | tf_op jit(solution)/shard_map/jit(_solve_triangular)/triangular_solve | solution.py:40
  538.1 2.9 slice_subtract_fusion.4
  542.7 11.7 %custom-call.58 = f32[128,128]{1,0:T(8,128)S(1)} custom-call(f32[128,128]{1,0:T(8,128)S(1)} %slice.296), custom_call_target="Cholesky" | custom-call | tf_op jit(solution)/shard_map/cholesky/custom-call.1 | solution.py:39
  556.5 9.8 custom-call.59
  569.3 2.2 convolution_subtract_fusion.1
  572.6 11.9 %custom-call.60 = f32[128,128]{1,0:T(8,128)S(1)} custom-call(f32[128,128]{1,0:T(8,128)S(1)} %slice.299), custom_call_target="Cholesky" | custom-call | tf_op jit(solution)/shard_map/cholesky/custom-call.1 | solution.py:39
  586.5 9.8 custom-call.61
  601.1 13.2 %custom-call.62 = f32[128,128]{1,0:T(8,128)} custom-call(f32[128,128]{1,0:T(8,128)} %slice.302), custom_call_target="Cholesky" | custom-call | tf_op jit(solution)/shard_map/cholesky/custom-call.1 | solution.py:39
  615.9 2.2 select_bitcast_fusion.3
  618.0 11.3 %custom-call.63 = f32[1,128,128]{1,2,0:T(8,128)} custom-call(f32[1,128,128]{2,1,0:T(8,128)} %get-tuple-element.19), custom_call_target="InvertDiagBlocksLowerTriangular" | custom-call | tf_op jit(solution)/shard_map/jit(_solve_triangular)/triangular_solve | solution.py:40
  635.1 13.2 %custom-call.64 = f32[128,128]{1,0:T(8,128)} custom-call(f32[128,128]{1,0:T(8,128)} %slice.305), custom_call_target="Cholesky" | custom-call | tf_op jit(solution)/shard_map/cholesky/custom-call.1 | solution.py:39
  651.8 11.3 %custom-call.65 = f32[1,128,128]{1,2,0:T(8,128)} custom-call(f32[1,128,128]{2,1,0:T(8,128)} %get-tuple-element.17), custom_call_target="InvertDiagBlocksLowerTriangular" | custom-call | tf_op jit(solution)/shard_map/jit(_solve_triangular)/triangular_solve | solution.py:40
  674.4 13.2 %custom-call.66 = f32[128,128]{1,0:T(8,128)} custom-call(f32[128,128]{1,0:T(8,128)} %convolution_subtract_fusion.7), custom_call_target="Cholesky" | custom-call | tf_op jit(solution)/shard_map/cholesky/custom-call.1 | solution.py:39
  689.1 2.1 select_bitcast_fusion.1
  691.2 11.6 %custom-call.67 = f32[1,128,128]{1,2,0:T(8,128)} custom-call(f32[1,128,128]{2,1,0:T(8,128)} %get-tuple-element.15), custom_call_target="InvertDiagBlocksLowerTriangular" | custom-call | tf_op jit(solution)/shard_map/jit(_solve_triangular)/triangular_solve | solution.py:40
  717.5 2.8 convolution_negate_fusion
  720.4 20.0 %fusion.9 = bf16[1024,1024]{1,0:T(8,128)(2,1)} fusion(f32[1,1024,1024]{1,2,0:T(8,128)} %all-gather.16.cloned.1.call-done, f32[512,512]{1,0:T(8,128)} %copy-done.31, f32[128,128]{1,0:T(8,128)} %copy.12, f32[128,128]{1,0:T(8,128)} %copy-done.77, f32[128,256]{1,0:T(8,128)} %concatenate.225, f32[256,256]{1,0:T(8,128)} %copy-done.71, f32[256,512]{1,0:T(8,128)} %copy-done.61, ...), kind=kOutput, calls=%fused_computation.26 | convolution fusion | flops 12894339072 | bytes 9437184 | tf_op jit(solution)/shard_map/dot_general | solution.py:27
  740.3 23.0 %bitcast_select_fusion = f32[3968,1024]{1,0:T(8,128)} fusion(f32[1024,3968]{0,1:T(8,128)} %get-tuple-element.64, f32[3968,1024]{1,0:T(8,128)} %bitcast.190, pred[]{:T(512)S(6)} %eq.47, bf16[3968,1024]{1,0:T(8,128)(2,1)} %all-reduce.21.cloned.1.call-done, bf16[1024,1024]{1,0:T(8,128)(2,1)} %fusion.9), kind=kOutput, calls=%fused_computation.2 | convolution fusion | flops 8329625600 | bytes 58982400 | tf_op jit(solution)/shard_map/dot_general | solution.py:107
  763.4 31.3 %convert_select_fusion = (bf16[3840,1024]{1,0:T(8,128)(2,1)}, f32[3840,1024]{1,0:T(8,128)}) fusion(pred[]{:T(512)S(6)} %eq.49, f32[512,512]{1,0:T(8,128)} %select_maximum_fusion.2, f32[128,128]{1,0:T(8,128)} %copy.27, f32[128,128]{1,0:T(8,128)} %copy-done.81, f32[128,256]{1,0:T(8,128)} %concatenate.258, f32[256,256]{1,0:T(8,128)} %copy-done.72, ...), kind=kOutput, calls=%fused_computation.8 | convolution fusion | flops 24175443968 | bytes 42467328 | tf_op jit(solution)/shard_map/dot_general | solution.py:17
  801.5 4.4 fusion.249
  805.9 17.2 %fusion.3 = bf16[1024,1024]{1,0:T(8,128)(2,1)} fusion(f32[1024,1024]{1,0:T(8,128)} %fusion.249, f32[1,1024,1024]{2,1,0:T(8,128)} %all-gather.18.cloned.1.call-done, f32[512,512]{1,0:T(8,128)S(1)} %copy-done.32, f32[128,128]{1,0:T(8,128)S(1)} %copy-done.86, f32[128,128]{1,0:T(8,128)S(1)} %copy-done.82, f32[128,256]{1,0:T(8,128)S(1)} %copy-done.67, ...), kind=kOutput, calls=%fused_computation.13 | convolution fusion | flops 12894339072 | bytes 13631488 | tf_op jit(solution)/shard_map/dot_general | solution.py:27
  824.4 117.3 %all-reduce.23.cloned.1.call-done = bf16[3840,1024]{1,0:T(8,128)(2,1)} async-done(((bf16[3840,1024]{1,0:T(8,128)(2,1)}), bf16[3840,1024]{1,0:T(8,128)(2,1)}) %all-reduce.23.cloned.1.call-update) | async-done | bytes 7864336 | tf_op jit(solution)/shard_map/psum | solution.py:13
  941.7 20.8 %fusion = f32[3840,1024]{1,0:T(8,128)} fusion(f32[3840,1024]{1,0:T(8,128)} %get-tuple-element.66, f32[3968,1024]{1,0:T(8,128)} %bitcast_select_fusion, bf16[3840,1024]{1,0:T(8,128)(2,1)} %all-reduce.23.cloned.1.call-done, pred[]{:T(512)S(6)} %gt.3, pred[]{:T(512)S(6)} %eq.49, bf16[1024,1024]{1,0:T(8,128)(2,1)} %fusion.3), kind=kOutput, calls=%fused_computation.4 | convolution fusion | flops 8064860160 | bytes 57147392 | tf_op jit(solution)/shard_map/dot_general | solution.py:107
  962.5 11.2 %pad_maximum_fusion = f32[4096,1024]{1,0:T(8,128)} fusion(f32[3840,1024]{1,0:T(8,128)} %fusion, f32[128,1024]{1,0:T(8,128)S(1)} %slice_select_fusion, f32[128,1024]{1,0:T(8,128)S(1)} %dynamic-slice_select_fusion), kind=kLoop, calls=%fused_computation.1 | loop fusion | flops 8388608 | bytes 33554432 | tf_op jit(solution)/shard_map/concatenate | solution.py:119
  (382 shorter events, 129.6 us)
Async XLA Ops:
  6.5 49.7 %all-reduce.25.cloned.1.call-start = ((), (), s32[]{:S(2)}) async-start(), calls=%async_computation.7 | async-start | bytes 3145728 | tf_op jit(solution)/shard_map/psum | solution.py:13
  8.9 49.6 %copy-start.8 = (f32[1,128,1024]{1,2,0:T(8,128)}, f32[1,128,1024]{1,2,0:T(8,128)S(1)}, u32[]{:S(2)}) copy-start(f32[1,128,1024]{1,2,0:T(8,128)S(1)} %copy.46) | copy-start | bytes 1572868
  11.2 121.1 %all-gather.10.cloned.1.call-start = ((), (), s32[]{:S(2)}) async-start(), calls=%async_computation | async-start | bytes 4718592 | tf_op jit(solution)/shard_map/all_gather | solution.py:78
  56.3 350.8 %all-gather.12.cloned.1.call-start = ((), (), s32[]{:S(2)}) async-start(), calls=%async_computation.3 | async-start | bytes 4718592 | tf_op jit(solution)/shard_map/all_gather | solution.py:78
  58.6 348.5 %all-gather.14.cloned.1.call-start = ((), (), s32[]{:S(2)}) async-start(), calls=%async_computation.4 | async-start | bytes 4718592 | tf_op jit(solution)/shard_map/all_gather | solution.py:78
  59.2 661.2 %all-gather.16.cloned.1.call-start = ((), (), s32[]{:S(2)}) async-start(), calls=%async_computation.5 | async-start | bytes 4718592 | tf_op jit(solution)/shard_map/all_gather | solution.py:78
  59.7 680.6 %all-reduce.21.cloned.1.call-start = ((), (), s32[]{:S(2)}) async-start(), calls=%async_computation.1 | async-start | bytes 16252928 | tf_op jit(solution)/shard_map/psum | solution.py:13
  157.2 213.1 %copy-start.44 = (f32[128,128]{1,0:T(8,128)}, f32[128,128]{1,0:T(8,128)S(1)}, u32[]{:S(2)}) copy-start(f32[128,128]{1,0:T(8,128)S(1)} %get-tuple-element.46) | copy-start | bytes 196612
  189.0 178.4 %copy-start.45 = (f32[128,128]{1,0:T(8,128)}, f32[128,128]{1,0:T(8,128)S(1)}, u32[]{:S(2)}) copy-start(f32[128,128]{1,0:T(8,128)S(1)} %get-tuple-element.44) | copy-start | bytes 196612
  262.5 23.0 %copy-start.15 = (f32[512,512]{1,0:T(8,128)}, f32[512,512]{1,0:T(8,128)S(1)}, u32[]{:S(2)}) copy-start(f32[512,512]{1,0:T(8,128)S(1)} %convolution_subtract_fusion.2) | copy-start | bytes 3145732
  275.8 92.1 %copy-start.47 = (f32[128,128]{1,0:T(8,128)}, f32[128,128]{1,0:T(8,128)S(1)}, u32[]{:S(2)}) copy-start(f32[128,128]{1,0:T(8,128)S(1)} %get-tuple-element.38) | copy-start | bytes 196612
  302.7 66.5 %copy-start.40 = (f32[128,128]{1,0:T(8,128)}, f32[128,128]{1,0:T(8,128)S(1)}, u32[]{:S(2)}) copy-start(f32[128,128]{1,0:T(8,128)S(1)} %get-tuple-element.36) | copy-start | bytes 196612
  339.8 32.4 %copy-start.22 = (f32[128,128]{1,0:T(8,128)}, f32[128,128]{1,0:T(8,128)S(1)}, u32[]{:S(2)}) copy-start(f32[128,128]{1,0:T(8,128)S(1)} %fusion.208) | copy-start | bytes 196612
  353.4 13.6 %copy-start.57 = (f32[128,128]{1,0:T(8,128)}, f32[128,128]{1,0:T(8,128)S(1)}, u32[]{:S(2)}) copy-start(f32[128,128]{1,0:T(8,128)S(1)} %copy.10) | copy-start | bytes 196612
  366.2 3.5 copy-start.55
  366.7 3.5 copy-start.74
  366.7 3.5 copy-start.88
  366.8 8.2 copy-start.61
  367.4 4.8 copy-start.27
  367.8 4.3 copy-start.9
  370.2 4.8 copy-start.31
  372.7 38.9 %copy-start.77 = (f32[128,128]{1,0:T(8,128)}, f32[128,128]{1,0:T(8,128)S(1)}, u32[]{:S(2)}) copy-start(f32[128,128]{1,0:T(8,128)S(1)} %convolution_negate_fusion.10) | copy-start | bytes 196612
  373.1 38.5 %copy-start.71 = (f32[256,256]{1,0:T(8,128)}, f32[256,256]{1,0:T(8,128)S(1)}, u32[]{:S(2)}) copy-start(f32[256,256]{1,0:T(8,128)S(1)} %convolution_negate_fusion.4) | copy-start | bytes 786436
  410.8 395.1 %all-gather.18.cloned.1.call-start = ((), (), s32[]{:S(2)}) async-start(), calls=%async_computation.6 | async-start | bytes 4718592 | tf_op jit(solution)/shard_map/all_gather | solution.py:78
  411.6 530.1 %all-reduce.23.cloned.1.call-start = ((), (), s32[]{:S(2)}) async-start(), calls=%async_computation.2 | async-start | bytes 15728640 | tf_op jit(solution)/shard_map/psum | solution.py:13
  411.7 20.8 %copy-start.92 = (f32[1,1024,1024]{1,2,0:T(8,128)S(1)}, f32[1,1024,1024]{1,2,0:T(8,128)}, u32[]{:S(2)}) copy-start(f32[1,1024,1024]{1,2,0:T(8,128)} %all-gather.12.cloned.1.call-done) | copy-start | bytes 12582916
  473.0 7.5 copy-start.25
  505.2 21.0 %copy-start.35 = (f32[128,128]{0,1:T(8,128)}, f32[128,128]{0,1:T(8,128)S(1)}, u32[]{:S(2)}) copy-start(f32[128,128]{0,1:T(8,128)S(1)} %fusion.100) | copy-start | bytes 196612
  566.6 29.7 %copy-start.33 = (f32[128,128]{0,1:T(8,128)}, f32[128,128]{0,1:T(8,128)S(1)}, u32[]{:S(2)}) copy-start(f32[128,128]{0,1:T(8,128)S(1)} %fusion.96) | copy-start | bytes 196612
  630.6 3.2 copy-start.34
  706.1 6.1 copy-start.26
  706.1 6.1 copy-start.53
  706.1 6.1 copy-start.54
  706.1 7.2 copy-start.10
  706.1 7.2 copy-start.18
  706.1 7.2 copy-start.42
  706.1 7.2 copy-start.51
  706.1 7.2 copy-start.56
  706.1 7.6 copy-start.13
  706.1 7.6 copy-start.28
  706.1 7.6 copy-start.38
  706.2 7.6 copy-start.49
  706.2 7.6 copy-start.50
  706.2 7.6 copy-start.69
  706.2 7.6 copy-start.78
  706.2 7.6 copy-start.90
  708.4 8.2 copy-start.62
  794.7 3.4 copy-start.14
  794.7 3.4 copy-start.39
  794.7 3.4 copy-start.89
  794.8 3.4 copy-start.91
  794.8 3.6 copy-start.11
  794.8 3.6 copy-start.48
  794.8 3.6 copy-start.52
  795.9 2.6 copy-start.19
  795.9 2.6 copy-start.41
  798.2 2.9 copy-start.95
  798.2 3.2 copy-start.96
  801.4 4.5 copy-start.32
  801.4 4.5 copy-start.63
  801.5 4.5 copy-start.67
  801.5 4.5 copy-start.73
  801.5 4.5 copy-start.82
  801.5 4.5 copy-start.86
  (42 other events, 68.1 us)
Sparse Core Ops, SparseCore 0:
  11.3 44.8 all-reduce.24
  58.3 73.9 all-gather.9
  134.3 73.1 all-gather.11
  209.4 74.1 all-gather.13
  285.4 73.3 all-gather.15
  411.0 149.8 all-reduce.20
  563.0 72.3 all-gather.17
  794.8 146.8 all-reduce.22
where the time goes:
time: 993 us; the launch traced here: 981 us
  other arithmetic  423 us (43%)
  matrix products  258 us (26%)
  waiting for transfers between devices  225 us (23%)
  local copies, waits for them, and re-layouts  58.5 us (6%)
  between operations  16.1 us (2%)
    another operation x48, other arithmetic, factor_and_inverse(): small = lax.linalg.cholesky(rest[:width, :width], symmetrize_input=False)  207 us
    another operation x32, other arithmetic, factor_and_inverse(): inverse = jax.scipy.linalg.solve_triangular(small, identity, lower=True)  183 us
    psum x3, waiting for transfers between devices, from_root(): return lax.psum(jnp.where(mine, x, jnp.zeros_like(x)), axis)  162 us
    dot_general x30, matrix products, nt(): lax.dot_general(left, right, (((1,), (1,)), ((), ())), precision=precisio...  117 us
    dot_general x31, matrix products, nn(): lax.dot_general(left, right, (((1,), (0,)), ((), ())), precision=HIGHEST,...  80.8 us
    all_gather x5, waiting for transfers between devices, gather_rows(): return lax.all_gather(piece, 'row', axis=0, tiled=True)  60.6 us
    dot_general x2, matrix products, plain(): lax.dot_general(left, right, (((1,), (0,)), ((), ())), preferred_element_...  43.8 us
    unnamed x196, local copies, waits for them, and re-layouts  21.4 us
  transfers between devices with their start and end apart: 8, of which 3 were waited for; matrix products, arithmetic and copies ran while one was open for 70% of the time, Pallas kernels for 0%

commit v1 on v0

--- a/solution.py
+++ b/solution.py
@@ -8,9 +8,15 @@
 HIGHEST = lax.Precision.HIGHEST
 
 
+def add_all(value, name):
+    parts = lax.all_gather(value, name, axis=0, tiled=False)
+    summed = parts.sum(axis=0)
+    return summed
+
+
 def from_root(x, axis, root):
     mine = lax.axis_index(axis) == root
-    return lax.psum(jnp.where(mine, x, jnp.zeros_like(x)), axis)
+    return add_all(jnp.where(mine, x, jnp.zeros_like(x)), axis)
 
 
 def nt(left, right, precision=None):

time: 993 us -> 1080 us (1.088)
  waiting for transfers between devices: 225 us -> 272 us
  other arithmetic: 423 us -> 469 us
    all_gather x0 -> x4, waiting for transfers between devices: none -> 212 us  [add_all(): parts = lax.all_gather(value, name, axis=0, tiled=False)]
    psum x3 -> x0, waiting for transfers between devices: 162 us -> none  [from_root(): return lax.psum(jnp.where(mine, x, jnp.zeros_like(x)), axis)]
    reduce_sum x0 -> x4, other arithmetic: none -> 36.1 us  [add_all(): summed = parts.sum(axis=0)]
  transfers between devices with their start and end apart: 8 -> 9, of which waited for: 3 -> 4; matrix products, arithmetic and copies ran while one was open for 70% -> 67% of each run, Pallas kernels for 0% -> 0%
where the time goes in v1:
time: 1080 us; the launch traced here: 1070 us
  other arithmetic  469 us (43%)
  waiting for transfers between devices  272 us (25%)
  matrix products  260 us (24%)
  local copies, waits for them, and re-layouts  56.8 us (5%)
  between operations  15.2 us (1%)
    all_gather x4, waiting for transfers between devices, add_all(): parts = lax.all_gather(value, name, axis=0, tiled=False)  212 us
    another operation x48, other arithmetic, factor_and_inverse(): small = lax.linalg.cholesky(rest[:width, :width], symmetrize_input=False)  206 us
    another operation x32, other arithmetic, factor_and_inverse(): inverse = jax.scipy.linalg.solve_triangular(small, identity, lower=True)  184 us
    dot_general x30, matrix products, nt(): lax.dot_general(left, right, (((1,), (1,)), ((), ())), precision=precisio...  117 us
    dot_general x31, matrix products, nn(): lax.dot_general(left, right, (((1,), (0,)), ((), ())), precision=HIGHEST,...  82.4 us
    all_gather x5, waiting for transfers between devices, gather_rows(): return lax.all_gather(piece, 'row', axis=0, tiled=True)  57.8 us
    dot_general x2, matrix products, plain(): lax.dot_general(left, right, (((1,), (0,)), ((), ())), preferred_element_...  43.2 us
    reduce_sum x4, other arithmetic, add_all(): summed = parts.sum(axis=0)  36.1 us
  transfers between devices with their start and end apart: 9, of which 4 were waited for; matrix products, arithmetic and copies ran while one was open for 67% of the time, Pallas kernels for 0%

profile of v1, /device:TPU:1, one launch (start us, length us, event | category | flops | bytes accessed | tf_op | source)
XLA Modules:
  0.0 1073.2 jit_solution(7713912423588243692)
XLA Ops:
  6.5 2.5 fusion.245
  11.5 22.7 %all-gather.17.cloned.1.call-done = f32[4,128,1024]{2,1,0:T(8,128)} async-done(((f32[1,128,1024]{2,1,0:T(8,128)}), f32[4,128,1024]{2,1,0:T(8,128)}) %all-gather.17.cloned.1.call-update) | async-done | bytes 2097168 | tf_op jit(solution)/shard_map/all_gather | solution.py:12
  37.2 33.1 %all-gather.21.cloned.1.call-done = f32[8,128,1024]{2,1,0:T(8,128)} async-done(((f32[2,128,1024]{2,1,0:T(8,128)}), f32[8,128,1024]{2,1,0:T(8,128)}) %all-gather.21.cloned.1.call-update) | async-done | bytes 4194320 | tf_op jit(solution)/shard_map/all_gather | solution.py:12
  70.3 2.7 reduce_sum.43
  76.2 11.9 %slice.227 = f32[31,128,1024]{2,1,0:T(8,128)} slice(f32[32,128,1024]{2,1,0:T(8,128)} %param.4), slice={[1:32], [0:128], [0:1024]} | slice | bytes 32505856 | tf_op jit(solution)/shard_map/slice | solution.py:96
  88.1 57.8 %all-gather.19.cloned.1.call-done = f32[1024,1024]{0,1:T(8,128)} async-done(((f32[128,1024]{0,1:T(8,128)}), f32[1024,1024]{0,1:T(8,128)}) %all-gather.19.cloned.1.call-update) | async-done | bytes 4194320 | tf_op jit(solution)/shard_map/all_gather | solution.py:84
  145.9 5.6 copy.29
  151.5 4.6 fusion.7
  158.1 11.7 %custom-call.36 = f32[128,128]{1,0:T(8,128)S(1)} custom-call(f32[128,128]{1,0:T(8,128)S(1)} %slice.260), custom_call_target="Cholesky" | custom-call | tf_op jit(solution)/shard_map/cholesky/custom-call.1 | solution.py:45
  171.1 9.8 custom-call.37
  182.8 4.9 slice_subtract_fusion.1
  189.4 11.9 %custom-call.38 = f32[128,128]{1,0:T(8,128)S(1)} custom-call(f32[128,128]{1,0:T(8,128)S(1)} %slice.263), custom_call_target="Cholesky" | custom-call | tf_op jit(solution)/shard_map/cholesky/custom-call.1 | solution.py:45
  202.7 9.8 custom-call.39
  214.2 3.7 slice_subtract_fusion.3
  219.3 11.7 %custom-call.40 = f32[128,128]{1,0:T(8,128)S(1)} custom-call(f32[128,128]{1,0:T(8,128)S(1)} %slice.266), custom_call_target="Cholesky" | custom-call | tf_op jit(solution)/shard_map/cholesky/custom-call.1 | solution.py:45
  233.1 10.2 custom-call.41
  245.0 2.9 slice_subtract_fusion.5
  249.1 11.7 %custom-call.42 = f32[128,128]{1,0:T(8,128)S(1)} custom-call(f32[128,128]{1,0:T(8,128)S(1)} %slice.269), custom_call_target="Cholesky" | custom-call | tf_op jit(solution)/shard_map/cholesky/custom-call.1 | solution.py:45
  262.8 9.8 custom-call.43
  276.4 11.9 %custom-call.44 = f32[128,128]{1,0:T(8,128)S(1)} custom-call(f32[128,128]{1,0:T(8,128)S(1)} %slice.272), custom_call_target="Cholesky" | custom-call | tf_op jit(solution)/shard_map/cholesky/custom-call.1 | solution.py:45
  290.2 9.8 custom-call.45
  304.3 11.7 %custom-call.46 = f32[128,128]{1,0:T(8,128)S(1)} custom-call(f32[128,128]{1,0:T(8,128)S(1)} %slice.275), custom_call_target="Cholesky" | custom-call | tf_op jit(solution)/shard_map/cholesky/custom-call.1 | solution.py:45
  317.3 9.8 custom-call.47
  330.7 11.7 %custom-call.48 = f32[128,128]{1,0:T(8,128)S(1)} custom-call(f32[128,128]{1,0:T(8,128)S(1)} %slice.278), custom_call_target="Cholesky" | custom-call | tf_op jit(solution)/shard_map/cholesky/custom-call.1 | solution.py:45
  344.3 9.8 custom-call.49
  357.4 11.7 %custom-call.50 = f32[128,128]{1,0:T(8,128)S(1)} custom-call(f32[128,128]{1,0:T(8,128)S(1)} %convolution_subtract_fusion.8), custom_call_target="Cholesky" | custom-call | tf_op jit(solution)/shard_map/cholesky/custom-call.1 | solution.py:45
  371.1 10.2 custom-call.51
  391.4 31.0 %bitcast_convert_fusion = (bf16[3968,1024]{1,0:T(8,128)(2,1)}, f32[1024,3968]{0,1:T(8,128)}) fusion(f32[3968,1024]{1,0:T(8,128)} %bitcast.192, f32[512,512]{1,0:T(8,128)S(1)} %select_maximum_fusion.3, f32[128,128]{1,0:T(8,128)S(1)} %copy-done.77, f32[128,128]{1,0:T(8,128)S(1)} %convolution_negate_fusion.10, f32[128,256]{1,0:T(8,128)S(1)} %copy-done.61, ...), kind=kOutput, calls=%fused_computation.3 | convolution fusion | flops 24976949248 | bytes 43778048 | tf_op jit(solution)/shard_map/dot_general | solution.py:23
  422.4 3.7 broadcast_select_fusion
  427.0 20.2 %fusion.9 = bf16[1024,1024]{1,0:T(8,128)(2,1)} fusion(f32[1,1024,1024]{2,1,0:T(8,128)} %all-gather.29.cloned.1.call-done, f32[512,512]{1,0:T(8,128)} %copy-done.28, f32[128,128]{1,0:T(8,128)S(1)} %copy-done.78, f32[128,128]{1,0:T(8,128)S(1)} %convolution_negate_fusion.10, f32[128,256]{1,0:T(8,128)S(1)} %copy-done.62, ...), kind=kOutput, calls=%fused_computation.26 | convolution fusion | flops 12894339072 | bytes 9437184 | tf_op jit(solution)/shard_map/dot_general | solution.py:33
  447.2 19.5 %convolution_convert_fusion = bf16[1024,1024]{1,0:T(8,128)(2,1)S(1)} fusion(f32[1024,1024]{1,0:T(8,128)S(1)} %bitcast.196, f32[512,512]{1,0:T(8,128)} %copy-done.28, f32[128,128]{1,0:T(8,128)S(1)} %copy-done.78, f32[128,128]{1,0:T(8,128)S(1)} %convolution_negate_fusion.10, f32[128,256]{1,0:T(8,128)S(1)} %copy-done.62, ...), kind=kOutput, calls=%fused_computation.27 | convolution fusion | flops 12894339072 | bytes 9437184 | tf_op jit(solution)/shard_map/dot_general | solution.py:33
  468.1 4.7 convolution_subtract_fusion
  472.8 5.5 copy.44
  478.3 4.4 fusion.4
  484.9 11.7 %custom-call.52 = f32[128,128]{1,0:T(8,128)S(1)} custom-call(f32[128,128]{1,0:T(8,128)S(1)} %slice.287), custom_call_target="Cholesky" | custom-call | tf_op jit(solution)/shard_map/cholesky/custom-call.1 | solution.py:45
  498.6 9.8 custom-call.53
  510.3 4.8 slice_subtract_fusion
  516.9 11.9 %custom-call.54 = f32[128,128]{1,0:T(8,128)S(1)} custom-call(f32[128,128]{1,0:T(8,128)S(1)} %slice.290), custom_call_target="Cholesky" | custom-call | tf_op jit(solution)/shard_map/cholesky/custom-call.1 | solution.py:45
  530.8 9.8 custom-call.55
  543.1 3.7 slice_subtract_fusion.2
  548.3 11.7 %custom-call.56 = f32[128,128]{1,0:T(8,128)S(1)} custom-call(f32[128,128]{1,0:T(8,128)S(1)} %slice.293), custom_call_target="Cholesky" | custom-call | tf_op jit(solution)/shard_map/cholesky/custom-call.1 | solution.py:45
  562.0 10.2 custom-call.57
  573.9 2.9 slice_subtract_fusion.4
  578.0 11.7 %custom-call.58 = f32[128,128]{1,0:T(8,128)S(1)} custom-call(f32[128,128]{1,0:T(8,128)S(1)} %slice.296), custom_call_target="Cholesky" | custom-call | tf_op jit(solution)/shard_map/cholesky/custom-call.1 | solution.py:45
  591.7 9.8 custom-call.59
  605.2 2.4 convolution_subtract_fusion.1
  608.7 11.9 %custom-call.60 = f32[128,128]{1,0:T(8,128)S(1)} custom-call(f32[128,128]{1,0:T(8,128)S(1)} %slice.299), custom_call_target="Cholesky" | custom-call | tf_op jit(solution)/shard_map/cholesky/custom-call.1 | solution.py:45
  622.6 9.8 custom-call.61
  637.2 13.2 %custom-call.62 = f32[128,128]{1,0:T(8,128)} custom-call(f32[128,128]{1,0:T(8,128)} %slice.302), custom_call_target="Cholesky" | custom-call | tf_op jit(solution)/shard_map/cholesky/custom-call.1 | solution.py:45
  654.0 11.5 %custom-call.63 = f32[1,128,128]{1,2,0:T(8,128)} custom-call(f32[1,128,128]{2,1,0:T(8,128)} %get-tuple-element.17), custom_call_target="InvertDiagBlocksLowerTriangular" | custom-call | tf_op jit(solution)/shard_map/jit(_solve_triangular)/triangular_solve | solution.py:46
  673.4 13.2 %custom-call.64 = f32[128,128]{1,0:T(8,128)} custom-call(f32[128,128]{1,0:T(8,128)} %slice.305), custom_call_target="Cholesky" | custom-call | tf_op jit(solution)/shard_map/cholesky/custom-call.1 | solution.py:45
  690.3 11.3 %custom-call.65 = f32[1,128,128]{1,2,0:T(8,128)} custom-call(f32[1,128,128]{2,1,0:T(8,128)} %get-tuple-element.15), custom_call_target="InvertDiagBlocksLowerTriangular" | custom-call | tf_op jit(solution)/shard_map/jit(_solve_triangular)/triangular_solve | solution.py:46
  706.2 13.2 %custom-call.66 = f32[128,128]{1,0:T(8,128)} custom-call(f32[128,128]{1,0:T(8,128)} %convolution_subtract_fusion.7), custom_call_target="Cholesky" | custom-call | tf_op jit(solution)/shard_map/cholesky/custom-call.1 | solution.py:45
  727.8 11.7 %custom-call.67 = f32[1,128,128]{1,2,0:T(8,128)} custom-call(f32[1,128,128]{2,1,0:T(8,128)} %get-tuple-element.13), custom_call_target="InvertDiagBlocksLowerTriangular" | custom-call | tf_op jit(solution)/shard_map/jit(_solve_triangular)/triangular_solve | solution.py:46
  754.9 2.8 convolution_negate_fusion
  757.8 16.0 %reduce_sum.44 = bf16[3968,1024]{1,0:T(8,128)(2,1)} reduce(bf16[4,3968,1024]{2,1,0:T(8,128)(2,1)} %bitcast.190, bf16[]{:T(256)} %constant.54.clone.1), dimensions={0}, to_apply=%region_4.7 | reduce | flops 12189696 | bytes 40632320 | tf_op jit(solution)/shard_map/reduce_sum | solution.py:13
  773.7 23.1 %bitcast_select_fusion = f32[3968,1024]{1,0:T(8,128)} fusion(f32[1024,3968]{0,1:T(8,128)} %get-tuple-element.63, f32[3968,1024]{1,0:T(8,128)} %bitcast.193, pred[]{:T(512)S(6)} %eq.47, bf16[3968,1024]{1,0:T(8,128)(2,1)} %reduce_sum.44, bf16[1024,1024]{1,0:T(8,128)(2,1)} %fusion.9), kind=kOutput, calls=%fused_computation.2 | convolution fusion | flops 8329625600 | bytes 58982400 | tf_op jit(solution)/shard_map/dot_general | solution.py:113
  796.9 31.3 %convert_select_fusion = (bf16[3840,1024]{1,0:T(8,128)(2,1)}, f32[3840,1024]{1,0:T(8,128)}) fusion(pred[]{:T(512)S(6)} %eq.49, f32[512,512]{1,0:T(8,128)} %select_maximum_fusion.2, f32[128,128]{1,0:T(8,128)} %copy.53, f32[128,128]{1,0:T(8,128)} %copy-done.73, f32[128,256]{1,0:T(8,128)} %concatenate.258, f32[256,256]{1,0:T(8,128)} %copy-done.66, ...), kind=kOutput, calls=%fused_computation.8 | convolution fusion | flops 24175443968 | bytes 42467328 | tf_op jit(solution)/shard_map/dot_general | solution.py:23
  839.0 4.9 fusion.249
  844.0 18.1 %fusion.3 = bf16[1024,1024]{1,0:T(8,128)(2,1)} fusion(f32[1024,1024]{1,0:T(8,128)} %fusion.249, f32[1,1024,1024]{2,1,0:T(8,128)} %all-gather.33.cloned.1.call-done, f32[512,512]{1,0:T(8,128)S(1)} %copy-done.27, f32[128,128]{1,0:T(8,128)S(1)} %copy-done.76, f32[128,128]{1,0:T(8,128)S(1)} %copy-done.74, f32[128,256]{1,0:T(8,128)S(1)} %copy-done.60, ...), kind=kOutput, calls=%fused_computation.13 | convolution fusion | flops 12894339072 | bytes 13631488 | tf_op jit(solution)/shard_map/dot_general | solution.py:33
  863.4 156.1 %all-gather.31.cloned.1.call-done = bf16[15360,1024]{1,0:T(8,128)(2,1)} async-done(((bf16[3840,1024]{1,0:T(8,128)(2,1)}), bf16[15360,1024]{1,0:T(8,128)(2,1)}) %all-gather.31.cloned.1.call-update) | async-done | bytes 31457296 | tf_op jit(solution)/shard_map/all_gather | solution.py:12
  1019.5 15.6 %reduce_sum.45 = bf16[3840,1024]{1,0:T(8,128)(2,1)} reduce(bf16[4,3840,1024]{2,1,0:T(8,128)(2,1)} %bitcast.191, bf16[]{:T(256)} %constant.54.clone.1), dimensions={0}, to_apply=%region_5.8 | reduce | flops 11796480 | bytes 39321600 | tf_op jit(solution)/shard_map/reduce_sum | solution.py:13
  1035.2 20.0 %fusion = f32[3840,1024]{1,0:T(8,128)} fusion(f32[3840,1024]{1,0:T(8,128)} %get-tuple-element.65, f32[3968,1024]{1,0:T(8,128)} %bitcast_select_fusion, bf16[3840,1024]{1,0:T(8,128)(2,1)} %reduce_sum.45, pred[]{:T(512)S(6)} %gt.3, pred[]{:T(512)S(6)} %eq.49, bf16[1024,1024]{1,0:T(8,128)(2,1)S(1)} %copy-done.88), kind=kOutput, calls=%fused_computation.4 | convolution fusion | flops 8064860160 | bytes 57147392 | tf_op jit(solution)/shard_map/dot_general | solution.py:113
  1055.2 11.2 %pad_maximum_fusion = f32[4096,1024]{1,0:T(8,128)} fusion(f32[3840,1024]{1,0:T(8,128)} %fusion, f32[128,1024]{1,0:T(8,128)S(1)} %slice_select_fusion.1, f32[128,1024]{1,0:T(8,128)S(1)} %dynamic-slice_select_fusion), kind=kLoop, calls=%fused_computation.1 | loop fusion | flops 8388608 | bytes 33554432 | tf_op jit(solution)/shard_map/concatenate | solution.py:125
  (372 shorter events, 147.9 us)
Async XLA Ops:
  6.5 27.7 %all-gather.17.cloned.1.call-start = ((), (), s32[]{:S(2)}) async-start(), calls=%async_computation | async-start | bytes 2621440 | tf_op jit(solution)/shard_map/all_gather | solution.py:12
  9.1 61.2 %all-gather.21.cloned.1.call-start = ((), (), s32[]{:S(2)}) async-start(), calls=%async_computation.2 | async-start | bytes 5242880 | tf_op jit(solution)/shard_map/all_gather | solution.py:12
  11.5 134.4 %all-gather.19.cloned.1.call-start = ((), (), s32[]{:S(2)}) async-start(), calls=%async_computation.1 | async-start | bytes 4718592 | tf_op jit(solution)/shard_map/all_gather | solution.py:84
  37.1 385.2 %all-gather.23.cloned.1.call-start = ((), (), s32[]{:S(2)}) async-start(), calls=%async_computation.3 | async-start | bytes 4718592 | tf_op jit(solution)/shard_map/all_gather | solution.py:84
  75.0 347.4 %all-gather.25.cloned.1.call-start = ((), (), s32[]{:S(2)}) async-start(), calls=%async_computation.4 | async-start | bytes 4718592 | tf_op jit(solution)/shard_map/all_gather | solution.py:84
  75.6 351.3 %all-gather.29.cloned.1.call-start = ((), (), s32[]{:S(2)}) async-start(), calls=%async_computation.6 | async-start | bytes 4718592 | tf_op jit(solution)/shard_map/all_gather | solution.py:84
  76.2 681.6 %all-gather.27.cloned.1.call-start = ((), (), s32[]{:S(2)}) async-start(), calls=%async_computation.5 | async-start | bytes 40632320 | tf_op jit(solution)/shard_map/all_gather | solution.py:12
  171.1 214.6 %copy-start.40 = (f32[128,128]{1,0:T(8,128)}, f32[128,128]{1,0:T(8,128)S(1)}, u32[]{:S(2)}) copy-start(f32[128,128]{1,0:T(8,128)S(1)} %get-tuple-element.44) | copy-start | bytes 196612
  202.7 180.1 %copy-start.41 = (f32[128,128]{1,0:T(8,128)}, f32[128,128]{1,0:T(8,128)S(1)}, u32[]{:S(2)}) copy-start(f32[128,128]{1,0:T(8,128)S(1)} %get-tuple-element.42) | copy-start | bytes 196612
  276.4 23.6 %copy-start.12 = (f32[512,512]{1,0:T(8,128)}, f32[512,512]{1,0:T(8,128)S(1)}, u32[]{:S(2)}) copy-start(f32[512,512]{1,0:T(8,128)S(1)} %convolution_subtract_fusion.2) | copy-start | bytes 3145732
  317.3 67.3 %copy-start.37 = (f32[128,128]{1,0:T(8,128)}, f32[128,128]{1,0:T(8,128)S(1)}, u32[]{:S(2)}) copy-start(f32[128,128]{1,0:T(8,128)S(1)} %get-tuple-element.34) | copy-start | bytes 196612
  327.5 27.1 %copy-start.50 = (f32[128,128]{1,0:T(8,128)}, f32[128,128]{1,0:T(8,128)S(1)}, u32[]{:S(2)}) copy-start(f32[128,128]{1,0:T(8,128)S(1)} %copy.36) | copy-start | bytes 196612
  329.2 27.0 %copy-start.47 = (f32[128,128]{1,0:T(8,128)}, f32[128,128]{1,0:T(8,128)S(1)}, u32[]{:S(2)}) copy-start(f32[128,128]{1,0:T(8,128)S(1)} %convolution_negate_fusion.11) | copy-start | bytes 196612
  355.3 28.0 %copy-start.51 = (f32[128,128]{1,0:T(8,128)S(1)}, f32[128,128]{1,0:T(8,128)}, u32[]{:S(2)}) copy-start(f32[128,128]{1,0:T(8,128)} %copy-done.50) | copy-start | bytes 196612
  357.1 30.5 %copy-start.17 = (f32[128,128]{1,0:T(8,128)}, f32[128,128]{1,0:T(8,128)S(1)}, u32[]{:S(2)}) copy-start(f32[128,128]{1,0:T(8,128)S(1)} %fusion.208) | copy-start | bytes 196612
  382.3 2.9 copy-start.52
  382.8 4.8 copy-start.23
  383.3 4.3 copy-start.8
  385.6 4.8 copy-start.28
  426.1 417.9 %all-gather.33.cloned.1.call-start = ((), (), s32[]{:S(2)}) async-start(), calls=%async_computation.8 | async-start | bytes 4718592 | tf_op jit(solution)/shard_map/all_gather | solution.py:84
  426.9 592.7 %all-gather.31.cloned.1.call-start = ((), (), s32[]{:S(2)}) async-start(), calls=%async_computation.7 | async-start | bytes 39321600 | tf_op jit(solution)/shard_map/all_gather | solution.py:12
  427.0 20.2 %copy-start.83 = (f32[1,1024,1024]{2,1,0:T(8,128)S(1)}, f32[1,1024,1024]{2,1,0:T(8,128)}, u32[]{:S(2)}) copy-start(f32[1,1024,1024]{2,1,0:T(8,128)} %all-gather.25.cloned.1.call-done) | copy-start | bytes 12582916
  427.0 20.2 %copy-start.85 = (f32[512,512]{1,0:T(8,128)S(1)}, f32[512,512]{1,0:T(8,128)}, u32[]{:S(2)}) copy-start(f32[512,512]{1,0:T(8,128)} %copy-done.84) | copy-start | bytes 3145732
  447.2 20.9 %copy-start.82 = (f32[1,1024,1024]{1,2,0:T(8,128)S(1)}, f32[1,1024,1024]{1,2,0:T(8,128)}, u32[]{:S(2)}) copy-start(f32[1,1024,1024]{1,2,0:T(8,128)} %all-gather.23.cloned.1.call-done) | copy-start | bytes 12582916
  508.7 7.5 copy-start.21
  540.9 35.9 %copy-start.32 = (f32[128,128]{0,1:T(8,128)}, f32[128,128]{0,1:T(8,128)S(1)}, u32[]{:S(2)}) copy-start(f32[128,128]{0,1:T(8,128)S(1)} %fusion.100) | copy-start | bytes 196612
  572.4 35.2 %copy-start.31 = (f32[128,128]{1,0:T(8,128)}, f32[128,128]{1,0:T(8,128)S(1)}, u32[]{:S(2)}) copy-start(f32[128,128]{1,0:T(8,128)S(1)} %fusion.98) | copy-start | bytes 196612
  601.8 30.6 %copy-start.29 = (f32[128,128]{0,1:T(8,128)}, f32[128,128]{0,1:T(8,128)S(1)}, u32[]{:S(2)}) copy-start(f32[128,128]{0,1:T(8,128)S(1)} %fusion.96) | copy-start | bytes 196612
  742.8 7.2 copy-start.22
  742.8 7.2 copy-start.49
  742.8 8.3 copy-start.10
  742.8 8.3 copy-start.24
  742.8 8.3 copy-start.35
  742.8 8.3 copy-start.44
  742.8 8.3 copy-start.45
  742.8 8.3 copy-start.64
  742.8 8.3 copy-start.70
  742.8 8.3 copy-start.80
  751.2 3.7 copy-start.56
  828.2 3.9 copy-start.65
  828.2 5.8 copy-start.11
  828.2 5.8 copy-start.36
  828.2 5.8 copy-start.79
  828.3 5.7 copy-start.81
  828.3 6.7 copy-start.9
  828.3 6.7 copy-start.43
  828.3 6.7 copy-start.46
  830.2 5.7 copy-start.14
  830.2 5.7 copy-start.38
  830.2 5.7 copy-start.39
  832.1 4.8 copy-start.18
  832.1 4.8 copy-start.68
  832.1 4.8 copy-start.71
  832.1 5.9 copy-start.69
  834.0 4.1 copy-start.72
  834.0 5.0 copy-start.87
  834.0 5.0 copy-start.89
  839.0 5.0 copy-start.27
  839.0 5.0 copy-start.57
  839.0 5.0 copy-start.60
  839.0 5.0 copy-start.67
  839.0 5.0 copy-start.74
  839.0 5.0 copy-start.76
  1019.5 15.6 %copy-start.88 = (bf16[1024,1024]{1,0:T(8,128)(2,1)S(1)}, bf16[1024,1024]{1,0:T(8,128)(2,1)}, u32[]{:S(2)}) copy-start(bf16[1024,1024]{1,0:T(8,128)(2,1)} %fusion.3) | copy-start | bytes 6291460
  (35 other events, 53.9 us)
Sparse Core Ops, SparseCore 0:
  9.2 25.0 all-gather.16
  35.8 34.4 all-gather.20
  72.4 73.4 all-gather.18
  147.8 73.1 all-gather.22
  223.0 70.5 all-gather.24
  295.6 71.9 all-gather.28
  426.2 197.5 all-gather.26
  626.0 71.9 all-gather.32
  828.3 191.1 all-gather.30
